TPU v7x, 16 devices: a 4x2x1 block of a 4x4x4 slice. The times are simulated.
16 devices in a mesh: dp: 4 (over y, z, core), sp: 4 (over x).
Axes of the slice: x: 4, y: 2, z: 1, core: 2. Of those that a mesh axis runs over, the one named last changes fastest.
The devices are a block of a 4x4x4 slice.
Arguments:
- q: bfloat16 [128, 32, 160], P('dp'), parts along dimension 0
- k: bfloat16 [128, 4096, 8, 160], P('dp', 'sp'), parts along dimension 0
- v: bfloat16 [128, 4096, 8, 160], P('dp', 'sp'), parts along dimension 0
Outputs:
- q: bfloat16 [128, 32, 160], P('dp'), parts along dimension 0
There are 4 independent parts. A program takes and returns all parts, laid end to end along the dimension named above; each array names one.
All inputs are finite; a program needn't handle non-finite values.
Results may differ from a plain program's by a relative error of at most 0.012.
Values are sent between devices in bfloat16 or wider.
A program may use at most 1.5 GiB of HBM per device.

v0:
```python
import jax
import jax.numpy as jnp
from jax import lax
from jax.sharding import PartitionSpec as P


def einsum(form, a, b):
    return jnp.einsum(form, a.astype(jnp.float32), b.astype(jnp.float32))


def part_of(q, k, v):
    grouped = q.reshape(q.shape[0], k.shape[2], -1, q.shape[2])
    scores = einsum("bgsd,bugd->bgsu", grouped, k) * q.shape[2] ** -0.5
    high = jnp.max(scores, -1, keepdims=True)
    weights = jnp.exp(scores - high)
    seen = einsum("bgsu,bugd->bgsd", weights.astype(jnp.bfloat16), v)
    return jnp.concatenate([seen, jnp.sum(weights, -1, keepdims=True), high], -1)


def together(parts):
    seen, total, high = parts[..., :-2], parts[..., -2:-1], parts[..., -1:]
    scale = jnp.exp(high - jnp.max(high, 0))
    return (jnp.sum(seen * scale, 0) / jnp.sum(total * scale, 0)).astype(jnp.bfloat16)


def solution(mesh):
    def step(q, k, v):
        return together(lax.all_gather(part_of(q, k, v), "sp")).reshape(q.shape)

    return jax.shard_map(
        step,
        mesh=mesh,
        in_specs=(P("dp", None, None), P("dp", "sp", None, None), P("dp", "sp", None, None)),
        out_specs=P("dp", None, None),
        check_vma=False,
    )
```

profile of v0, /device:TPU:112, one launch (start us, length us, event | category | flops | bytes accessed | tf_op | source)
XLA Modules:
  0.0 145.9 jit_solution(13002648035824414195)
XLA Ops:
  6.5 0.0 all-gather.3.cloned.1.call-start
  6.6 1.2 reshape.15
  7.8 30.1 %multiply_reduce_fusion = (f32[32,8,4]{2,1,0:T(8,128)S(1)}, f32[32,8,4,1024]{3,2,1,0:T(4,128)}) fusion(bf16[32,8,4,160]{3,2,1,0:T(4,128)(2,1)S(1)} %reshape.15, bf16[32,1024,8,160]{1,3,2,0:T(8,128)(2,1)} %param.4), kind=kOutput, calls=%fused_computation.3 | convolution fusion | flops 337640448 | bytes 88412160 | tf_op jit(solution)/shard_map/bgsd,bugd->bgsu/dot_general | solution.py:8
  37.8 3.6 %fusion.1 = f32[32,8,4]{2,1,0:T(8,128)S(1)} fusion(f32[32,8,4,1024]{3,2,1,0:T(4,128)} %get-tuple-element.11, f32[32,8,4]{2,1,0:T(8,128)S(1)} %get-tuple-element.10), kind=kLoop, calls=%fused_computation.4 | loop fusion | flops 3144704 | bytes 4202496 | tf_op jit(solution)/shard_map/reduce_sum | solution.py:17
  41.4 32.0 %fusion.3 = f32[32,8,4,160]{3,2,1,0:T(4,128)S(1)} fusion(bf16[32,1024,8,160]{1,3,2,0:T(8,128)(2,1)} %param.5, f32[32,8,4,1024]{3,2,1,0:T(4,128)} %get-tuple-element.11, f32[32,8,4]{2,1,0:T(8,128)S(1)} %get-tuple-element.10), kind=kOutput, calls=%fused_computation.6 | convolution fusion | flops 338690048 | bytes 88739840 | tf_op jit(solution)/shard_map/bgsu,bugd->bgsd/dot_general | solution.py:8
  73.5 1.7 %copy.51 = f32[32,8,4,1]{3,2,1,0:T(4,128)S(1)} copy(f32[32,8,4,1]{2,1,0,3:T(8,128)S(1)} %bitcast.16) | data formatting | bytes 8192 | tf_op jit(solution)/shard_map/broadcast_in_dim | solution.py:17
  75.2 1.7 %copy.52 = f32[32,8,4,1]{3,2,1,0:T(4,128)S(1)} copy(f32[32,8,4,1]{2,1,0,3:T(8,128)S(1)} %bitcast.15) | data formatting | bytes 8192 | tf_op jit(solution)/shard_map/broadcast_in_dim | solution.py:14
  76.8 0.7 pad_maximum_fusion
  77.5 1.2 copy.53
  78.7 0.1 all-gather.3.cloned.1.call-update
  78.7 47.0 %all-gather.3.cloned.1.call-done = f32[128,8,4,162]{3,1,2,0:T(8,128)} async-done(((f32[32,8,4,162]{3,1,2,0:T(8,128)}), f32[128,8,4,162]{3,1,2,0:T(8,128)}) %all-gather.3.cloned.1.call-update) | async-done | bytes 2654224 | tf_op jit(solution)/shard_map/all_gather | solution.py:28
  125.7 4.7 %fusion.10 = (f32[4,32,8,4,1]{4,2,3,1,0:T(8,128)}, f32[32,8,4]{1,2,0:T(4,128)S(1)}, f32[4,32,8,4,1]{4,2,3,1,0:T(8,128)S(1)}) fusion(f32[4,32,8,4,162]{4,2,3,1,0:T(8,128)} %bitcast.13), kind=kLoop, calls=%fused_computation.17 | loop fusion | flops 3072 | bytes 69632 | tf_op jit(solution)/shard_map/slice | solution.py:21
  130.4 2.6 %copy.65 = f32[4,32,8,4,1]{1,2,4,3,0:T(8,128)S(1)} copy(f32[4,32,8,4,1]{4,2,3,1,0:T(8,128)} %get-tuple-element.5) | data formatting | bytes 32768
  133.0 0.1 copy.66
  133.1 1.1 copy.64
  134.3 0.1 copy.55
  134.4 2.7 %fusion = f32[32,8,4,160]{3,1,2,0:T(8,128)S(1)} fusion(f32[4,32,8,4,162]{4,2,3,1,0:T(8,128)} %bitcast.14, f32[4,32,8,4]{2,3,1,0:T(4,128)S(1)} %copy.55), kind=kLoop, calls=%fused_computation.1 | loop fusion | flops 1146880 | bytes 3293184 | tf_op jit(solution)/shard_map/reduce_sum | solution.py:23
  137.1 0.6 copy.56
  137.7 0.2 fusion.7
  137.9 1.1 copy.59
  (2 shorter events, 0.0 us)
Async XLA Ops:
  6.5 119.2 %all-gather.3.cloned.1.call-start = ((), (), s32[]{:S(2)}) async-start(), calls=%async_computation | async-start | bytes 5242880 | tf_op jit(solution)/shard_map/all_gather | solution.py:28
Sparse Core Ops, SparseCore 0:
  78.8 46.8 all-gather.2
where the time goes:
time: 146 us
  matrix products  62.1 us (43%)
  waiting for transfers between devices  47 us (32%)
  between operations  13.5 us (9%)
  other arithmetic  11.9 us (8%)
  local copies, waits for them, and re-layouts  11.4 us (8%)
    dot_general x2, matrix products, einsum(): return jnp.einsum(form, a.astype(jnp.float32), b.astype(jnp.float32))  62.1 us
    all_gather x1, waiting for transfers between devices, step(): return together(lax.all_gather(part_of(q, k, v), 'sp')).reshape(q.shape)  47 us
    slice x1, other arithmetic, together(): seen, total, high = (parts[..., :-2], parts[..., -2:-1], parts[..., -1:])  4.72 us
    unnamed x3, local copies, waits for them, and re-layouts  3.8 us
    reduce_sum x1, other arithmetic, part_of(): jnp.sum(weights, -1, keepdims=True)  3.62 us
  transfers between devices with their start and end apart: 1, of which 1 were waited for; matrix products, arithmetic and copies ran while one was open for 0% of the time, Pallas kernels for 0%

commit v1 on v0

v1 whole, which is shorter than its diff:
```python
import functools

import jax
import jax.numpy as jnp
from jax import lax
from jax.experimental import pallas as pl
from jax.experimental.pallas import tpu as pltpu
from jax.sharding import PartitionSpec as P

F32, BF16 = jnp.float32, jnp.bfloat16
SLOTS = 4
LANES = 128
LOG2E = 1.4426950408889634


def kernel(axis, n, dims, q_hbm, k_hbm, v_hbm, out_hbm, q_ref, k_buf, v_buf, w_ref, acc_ref, row_ref, parts, stats, out_ref, q_sem, k_sem, v_sem, send_sem, recv_sem, stat_send, stat_recv, out_sem):
    batch, heads, kv_heads, head, run = dims
    share = heads // kv_heads
    pack = LANES // heads
    chunks = batch // pack
    me = lax.axis_index(axis)
    scale = head**-0.5 * LOG2E

    barrier = pltpu.get_barrier_semaphore()
    for step in range(1, n):
        pl.semaphore_signal(barrier, inc=1, device_id={axis: lax.rem(me + step, n)}, device_id_type=pl.DeviceIdType.MESH)

    def q_copy():
        return pltpu.make_async_copy(q_hbm, q_ref, q_sem)

    def k_copy(i):
        return pltpu.make_async_copy(k_hbm.at[i], k_buf.at[lax.rem(i, SLOTS)], k_sem.at[lax.rem(i, SLOTS)])

    def v_copy(i):
        return pltpu.make_async_copy(v_hbm.at[i], v_buf.at[lax.rem(i, SLOTS)], v_sem.at[lax.rem(i, SLOTS)])

    q_copy().start()
    for i in range(SLOTS):
        k_copy(i).start()
        v_copy(i).start()

    own = lax.broadcasted_iota(jnp.int32, (heads, kv_heads * head), 0) // share
    col = lax.broadcasted_iota(jnp.int32, (heads, kv_heads * head), 1)
    diagonal = (col >= own * head) & (col < own * head + head)

    def scores(i):
        q = q_ref[i]
        wide = jnp.where(diagonal, jnp.concatenate([q] * kv_heads, axis=1), jnp.zeros((), BF16))
        return jnp.dot(wide, k_buf[lax.rem(i, SLOTS)], preferred_element_type=F32)

    def weigh(i, s):
        place = lax.rem(i, pack) * heads
        s = s * scale
        high = jnp.max(s, axis=1, keepdims=True)
        weights = jnp.exp2(s - high)
        total = jnp.sum(weights, axis=1, keepdims=True)
        w_ref[pl.ds(pl.multiple_of(place, heads), heads), :] = weights.astype(BF16)
        lane = lax.broadcasted_iota(jnp.int32, (heads, LANES), 1)
        row = lax.broadcasted_iota(jnp.int32, (heads, LANES), 0)
        here = lane == row + place
        line = lax.broadcasted_iota(jnp.int32, (1, LANES), 1)
        mine = (line >= place) & (line < place + heads)
        slot = lax.rem(i // pack, 2)
        high = jnp.sum(jnp.where(here, high, 0.0), axis=0, keepdims=True)
        total = jnp.sum(jnp.where(here, total, 0.0), axis=0, keepdims=True)
        row_ref[slot, 0:1, :] = jnp.where(mine, high, row_ref[slot, 0:1, :])
        row_ref[slot, 1:2, :] = jnp.where(mine, total, row_ref[slot, 1:2, :])

    def values(i):
        place = lax.rem(i, pack) * heads
        seen = lax.dot_general(v_buf[lax.rem(i, SLOTS)], w_ref[...], (((1,), (1,)), ((), ())), preferred_element_type=F32)
        lane = lax.broadcasted_iota(jnp.int32, (head, LANES), 1)
        acc = acc_ref[...]
        for g in range(kv_heads):
            first = place + g * share
            acc = jnp.where((lane >= first) & (lane < first + share), seen[g * head : (g + 1) * head], acc)
        acc_ref[...] = acc

    def part_copy(c, step):
        peer = lax.rem(me + step, n)
        return pltpu.make_async_remote_copy(
            parts.at[me, c], parts.at[me, c], send_sem.at[c, step - 1], recv_sem.at[c, step - 1],
            device_id={axis: peer}, device_id_type=pl.DeviceIdType.MESH)

    def stat_copy(c, step):
        peer = lax.rem(me + step, n)
        return pltpu.make_async_remote_copy(
            stats.at[me, c], stats.at[me, c], stat_send.at[c, step - 1], stat_recv.at[c, step - 1],
            device_id={axis: peer}, device_id_type=pl.DeviceIdType.MESH)

    def send(c):
        stats[me, c] = row_ref[lax.rem(c, 2)]
        parts[me, c] = acc_ref[...].astype(BF16)
        for step in range(1, n):
            stat_copy(c, step).start()
            part_copy(c, step).start()

    def out_copy(c):
        rows = pl.ds(pl.multiple_of(c * LANES, LANES), LANES)
        return pltpu.make_async_copy(out_ref.at[rows], out_hbm.at[rows], out_sem.at[c])

    def combine(c):
        for step in range(1, n):
            stat_copy(c, step).wait_recv()
            part_copy(c, step).wait_recv()
        high = [stats[d, c, 0:1, :] for d in range(n)]
        top = functools.reduce(jnp.maximum, high)
        factor = [jnp.exp2(h - top) for h in high]
        total = sum(stats[d, c, 1:2, :] * factor[d] for d in range(n))
        seen = sum(parts[d, c].astype(F32) * factor[d] for d in range(n)) / total
        rows = pl.ds(pl.multiple_of(c * LANES, LANES), LANES)
        out_ref[rows, :] = seen.T.astype(BF16)
        out_copy(c).start()

    row_ref[...] = jnp.zeros_like(row_ref)
    acc_ref[...] = jnp.zeros_like(acc_ref)
    q_copy().wait()
    k_copy(0).wait()
    weigh(0, scores(0))
    k_copy(SLOTS).start()
    pl.semaphore_wait(barrier, n - 1)

    def body(i, carry):
        k_copy(i).wait()
        v_copy(i - 1).wait()
        s = scores(i)
        values(i - 1)
        weigh(i, s)

        @pl.when(i + SLOTS < batch)
        def _():
            k_copy(i + SLOTS).start()

        @pl.when(i - 1 + SLOTS < batch)
        def _():
            v_copy(i - 1 + SLOTS).start()

        @pl.when(lax.rem(i, pack) == 0)
        def _():
            send(i // pack - 1)

        @pl.when((lax.rem(i, pack) == pack - 1) & (i > pack))
        def _():
            combine(i // pack - 1)

        return carry

    lax.fori_loop(1, batch, body, 0)
    v_copy(batch - 1).wait()
    values(batch - 1)
    send(chunks - 1)
    combine(chunks - 1)

    def finish(c, carry):
        for step in range(1, n):
            stat_copy(c, step).wait_send()
            part_copy(c, step).wait_send()
        out_copy(c).wait()
        return carry

    lax.fori_loop(0, chunks, finish, 0)


def solution(mesh):
    axis = "sp"
    n = mesh.shape[axis]

    def step(q, k, v):
        batch, heads, head = q.shape
        run, kv_heads = k.shape[1], k.shape[2]
        flat = (batch, kv_heads * head, run)
        k = k.transpose(0, 2, 3, 1).reshape(flat)
        v = v.transpose(0, 2, 3, 1).reshape(flat)
        chunks = batch * heads // LANES
        out = pl.pallas_call(
            functools.partial(kernel, axis, n, (batch, heads, kv_heads, head, run)),
            out_shape=jax.ShapeDtypeStruct((batch * heads, head), BF16),
            in_specs=[pl.BlockSpec(memory_space=pl.ANY)] * 3,
            out_specs=pl.BlockSpec(memory_space=pl.ANY),
            scratch_shapes=[
                pltpu.VMEM((batch, heads, head), BF16),
                pltpu.VMEM((SLOTS,) + flat[1:], BF16),
                pltpu.VMEM((SLOTS,) + flat[1:], BF16),
                pltpu.VMEM((LANES, run), BF16),
                pltpu.VMEM((head, LANES), F32),
                pltpu.VMEM((2, 8, LANES), F32),
                pltpu.VMEM((n, chunks, head, LANES), BF16),
                pltpu.VMEM((n, chunks, 8, LANES), F32),
                pltpu.VMEM((batch * heads, head), BF16),
                pltpu.SemaphoreType.DMA,
                pltpu.SemaphoreType.DMA((SLOTS,)),
                pltpu.SemaphoreType.DMA((SLOTS,)),
                pltpu.SemaphoreType.DMA((chunks, n - 1)),
                pltpu.SemaphoreType.DMA((chunks, n - 1)),
                pltpu.SemaphoreType.DMA((chunks, n - 1)),
                pltpu.SemaphoreType.DMA((chunks, n - 1)),
                pltpu.SemaphoreType.DMA((chunks,)),
            ],
            compiler_params=pltpu.CompilerParams(collective_id=0, has_side_effects=True, vmem_limit_bytes=60 * 2**20),
        )(q, k, v)
        return out.reshape(q.shape)

    return jax.shard_map(
        step,
        mesh=mesh,
        in_specs=(P("dp", None, None), P("dp", "sp", None, None), P("dp", "sp", None, None)),
        out_specs=P("dp", None, None),
        check_vma=False,
    )
```

time: 146 us -> 62.2 us (0.43)
  matrix products: 62.1 us -> 0 us
  Pallas kernels: 0 us -> 60.1 us
  waiting for transfers between devices: 47 us -> 0 us
  between operations: 13.5 us -> 0.01 us
  other arithmetic: 11.9 us -> 0 us
  local copies, waits for them, and re-layouts: 11.4 us -> 1.87 us
    dot_general x2 -> x0, matrix products: 62.1 us -> none  [einsum(): return jnp.einsum(form, a.astype(jnp.float32), b.astype(jnp.float32))]
    pallas_call x0 -> x1, Pallas kernels: none -> 60.1 us  [step(): pl.pallas_call(functools.partial(kernel, axis, n, (batch, heads, kv_heads...]
    all_gather x1 -> x0, waiting for transfers between devices: 47 us -> none  [step(): return together(lax.all_gather(part_of(q, k, v), 'sp')).reshape(q.shape)]
    reduce_sum x3 -> x0, other arithmetic: 6.3 us -> none  [the longest x1 3.62 us: part_of(): jnp.sum(weights, -1, keepdims=True)]
    slice x1 -> x0, other arithmetic: 4.72 us -> none  [together(): seen, total, high = (parts[..., :-2], parts[..., -2:-1], parts[..., -1:])]
    broadcast_in_dim x2 -> x0, local copies, waits for them, and re-layouts: 3.33 us -> none  [the longest x1 1.66 us: part_of(): jnp.sum(weights, -1, keepdims=True)]
    unnamed x3 -> x1, local copies, waits for them, and re-layouts: 3.8 us -> 1.87 us
  transfers between devices with their start and end apart: 1 -> 0, of which waited for: 1 -> 0; matrix products, arithmetic and copies ran while one was open for 0% -> 0% of each run, Pallas kernels for 0% -> 0%
where the time goes in v1:
time: 62.2 us; the launch traced here: 62 us
  Pallas kernels  60.1 us (97%)
  local copies, waits for them, and re-layouts  1.87 us (3%)
    pallas_call x1, Pallas kernels, step(): pl.pallas_call(functools.partial(kernel, axis, n, (batch, heads, kv_heads...  60.1 us
    unnamed x1, local copies, waits for them, and re-layouts  1.87 us

profile of v1, /device:TPU:112, one launch (start us, length us, event | category | flops | bytes accessed | tf_op | source)
XLA Modules:
  0.0 62.0 jit_solution(8920185794005017627)
XLA Ops:
  0.0 60.1 %shard_map.37 = bf16[1024,160]{1,0:T(8,128)(2,1)} custom-call(bf16[32,32,160]{2,1,0:T(8,128)(2,1)} %q_hbm.1, bf16[32,1280,1024]{2,1,0:T(8,128)(2,1)} %bitcast.1.k_hbm, bf16[32,1280,1024]{2,1,0:T(8,128)(2,1)} %bitcast.3.v_hbm), custom_call_target="tpu_custom_call" | custom-call | tf_op jit(solution)/shard_map/pallas_call | solution.py:175
  60.1 1.9 %copy.5 = bf16[32,32,160]{2,1,0:T(8,128)(2,1)} copy(bf16[32,32,160]{2,1,0:T(8,128)(2,1)} %bitcast.7) | data formatting | bytes 655360

commit v2 on v1

v2 whole, which is shorter than its diff:
```python
import functools

import jax
import jax.numpy as jnp
from jax import lax
from jax.experimental import pallas as pl
from jax.experimental.pallas import tpu as pltpu
from jax.sharding import PartitionSpec as P

F32, BF16 = jnp.float32, jnp.bfloat16
SLOTS = 4
VMEM_LIMIT = 33554432
LANES = 128
LOG2E = 1.4426950408889634


def rem(a, b):
    return a % b if isinstance(a, int) else lax.rem(a, b)


def fold(x):
    groups = LANES // x.shape[1]
    rows = x.shape[0] // groups
    return jnp.concatenate([x[j * rows : (j + 1) * rows] for j in range(groups)], axis=1)


def unfold(x, lanes):
    return jnp.concatenate([x[:, j * lanes : (j + 1) * lanes] for j in range(LANES // lanes)], axis=0)


def kernel(axis, n, dims, q_hbm, k_hbm, v_hbm, out_ref, q_ref, wide_ref, k_buf, v_buf, w_ref, acc_ref, row_ref, parts, stats, last_parts, last_stats, q_sem, k_sem, v_sem, half_sem, send_sem, recv_sem, last_send, last_recv):
    batch, heads, kv_heads, head, run = dims
    share = heads // kv_heads
    rest = head - LANES
    pack = LANES // heads
    solo = pack - 1
    main = batch - solo
    chunks = batch // pack
    me = lax.axis_index(axis)
    scale = head**-0.5 * LOG2E
    steps = sorted(range(1, n), key=lambda step: min(step, n - step))

    barrier = pltpu.get_barrier_semaphore()
    for step in steps:
        pl.semaphore_signal(barrier, inc=1, device_id={axis: lax.rem(me + step, n)}, device_id_type=pl.DeviceIdType.MESH)

    def q_copy():
        return pltpu.make_async_copy(q_hbm, q_ref, q_sem)

    def k_copy(i):
        return pltpu.make_async_copy(k_hbm.at[i], k_buf.at[lax.rem(i, SLOTS)], k_sem.at[lax.rem(i, SLOTS)])

    def v_half(i, j):
        rows = pl.ds(j * (kv_heads // 2) * head, (kv_heads // 2) * head)
        return pltpu.make_async_copy(v_hbm.at[i, rows], v_buf.at[i % SLOTS, rows], half_sem.at[j])

    def v_copy(i):
        return pltpu.make_async_copy(v_hbm.at[i], v_buf.at[lax.rem(i, SLOTS)], v_sem.at[lax.rem(i, SLOTS)])

    q_copy().start()
    for i in range(SLOTS):
        k_copy(i).start()
        v_copy(i).start()

    own = lax.broadcasted_iota(jnp.int32, (heads, kv_heads * head), 0) // share
    col = lax.broadcasted_iota(jnp.int32, (heads, kv_heads * head), 1)
    diagonal = (col >= own * head) & (col < own * head + head)

    def place_of(i):
        return rem(i + pack - 1, pack) * heads

    def chunk_of(i):
        return (i + pack - 1) // pack

    def remote(ref, send, recv, key, step):
        return pltpu.make_async_remote_copy(
            ref.at[(me, *key)], ref.at[(me, *key)], send.at[(*key, step - 1)], recv.at[(*key, step - 1)],
            device_id={axis: lax.rem(me + step, n)}, device_id_type=pl.DeviceIdType.MESH)

    def part_copy(c, step):
        return remote(parts, send_sem.at[0], recv_sem.at[0], (c,), step)

    def stat_copy(c, step):
        return remote(stats, send_sem.at[1], recv_sem.at[1], (c,), step)

    def last_part_copy(i, step):
        return remote(last_parts, last_send.at[0], last_recv.at[0], (i - main,), step)

    def last_stat_copy(i, step):
        return remote(last_stats, last_send.at[1], last_recv.at[1], (i - main,), step)

    def widen(i):
        wide_ref[...] = jnp.where(diagonal, jnp.concatenate([q_ref[i]] * kv_heads, axis=1), jnp.zeros((), BF16))

    def scores(i):
        return jnp.dot(wide_ref[...], k_buf[rem(i, SLOTS)], preferred_element_type=F32)

    def lines(here, high, total):
        return [jnp.sum(jnp.where(here, x, 0.0), axis=0, keepdims=True) for x in (high, total)]

    def weigh(i, s):
        place = place_of(i)
        s = s * scale
        high = jnp.max(s, axis=1, keepdims=True)
        weights = jnp.exp2(s - high)
        total = jnp.sum(weights, axis=1, keepdims=True)
        w_ref[pl.ds(pl.multiple_of(place, heads), heads), :] = weights.astype(BF16)
        lane = lax.broadcasted_iota(jnp.int32, (heads, LANES), 1)
        row = lax.broadcasted_iota(jnp.int32, (heads, LANES), 0)
        if isinstance(i, int) and i >= main:
            high, total = lines(lane == row, high, total)
            last_stats[me, i - main, 0:1, :] = high
            last_stats[me, i - main, 1:2, :] = total
            for step in steps:
                last_stat_copy(i, step).start()
        else:
            high, total = lines(lane == row + place, high, total)
            line = lax.broadcasted_iota(jnp.int32, (1, LANES), 1)
            mine = (line >= place) & (line < place + heads)
            slot = rem(chunk_of(i), 2)
            row_ref[slot, 0:1, :] = jnp.where(mine, high, row_ref[slot, 0:1, :])
            row_ref[slot, 1:2, :] = jnp.where(mine, total, row_ref[slot, 1:2, :])

    tile = 256
    depths, spans = kv_heads * head // tile, 2
    wide_span = run // spans

    def score_piece(i, j, total):
        depth, span = j % depths, j // depths
        piece = jnp.dot(
            wide_ref[:, depth * tile : (depth + 1) * tile],
            k_buf[rem(i, SLOTS), depth * tile : (depth + 1) * tile, span * wide_span : (span + 1) * wide_span],
            preferred_element_type=F32)
        return piece if total is None else total + piece

    def value_piece(i, j):
        g, span = j // spans, j % spans
        across = slice(span * wide_span, (span + 1) * wide_span)
        return lax.dot_general(
            v_buf[rem(i, SLOTS), g * head : (g + 1) * head, across], w_ref[:, across], (((1,), (1,)), ((), ())), preferred_element_type=F32)

    def take(i, g, seen, acc):
        lane = lax.broadcasted_iota(jnp.int32, (head, LANES), 1)
        first = place_of(i) + g * share
        return jnp.where((lane >= first) & (lane < first + share), seen, acc)

    def keep(i, acc):
        if isinstance(i, int) and i >= main:
            place = place_of(i)
            rows = acc.T[place : place + heads]
            last_parts[me, i - main, :heads, :] = rows[:, :LANES].astype(BF16)
            last_parts[me, i - main, heads:, :] = fold(rows[:, LANES:]).astype(BF16)
            for step in steps:
                last_part_copy(i, step).start()
        else:
            acc_ref[...] = acc

    def values(i, arrive=()):
        acc = acc_ref[...]
        for g in range(kv_heads):
            if arrive and g == kv_heads // 2:
                arrive[0].wait()
            acc = take(i, g, sum(value_piece(i, g * spans + j) for j in range(spans)), acc)
        keep(i, acc)

    def both(i):
        acc, seen, total = acc_ref[...], None, [None] * spans
        for j in range(kv_heads * spans):
            piece = value_piece(i - 1, j)
            seen = piece if j % spans == 0 else seen + piece
            if j % spans == spans - 1:
                acc = take(i - 1, j // spans, seen, acc)
            if j < depths * spans:
                total[j // depths] = score_piece(i, j, total[j // depths])
        return jnp.concatenate(total, axis=1), acc

    def send(c):
        stats[me, c] = row_ref[rem(c, 2)]
        parts[me, c] = acc_ref[...].astype(BF16)
        for step in steps:
            stat_copy(c, step).start()
            part_copy(c, step).start()

    def factors(lines_of):
        high, total = [[lines_of(d)[j : j + 1] for d in range(n)] for j in range(2)]
        top = functools.reduce(jnp.maximum, high)
        factor = [jnp.exp2(h - top) for h in high]
        total = sum(t * f for t, f in zip(total, factor))
        return [f / total for f in factor]

    def combine(c):
        for step in steps:
            stat_copy(c, step).wait_recv()
            part_copy(c, step).wait_recv()
        factor = factors(lambda d: stats[d, c])
        seen = sum(parts[d, c].astype(F32) * factor[d] for d in range(n)).T.astype(BF16)
        if isinstance(c, int) and c == 0:
            out_ref[:heads, :] = seen[LANES - heads :]
        else:
            out_ref[pl.ds(pl.multiple_of((c * pack - solo) * heads, heads), LANES), :] = seen

    def combine_last(i):
        for step in steps:
            last_stat_copy(i, step).wait_recv()
        factor = factors(lambda d: last_stats[d, i - main])
        columns = jnp.concatenate(factor + [jnp.zeros((8 - n, LANES), F32)], axis=0).T[:heads]
        major = [jnp.broadcast_to(columns[:, d : d + 1], (heads, LANES)) for d in range(n)]
        minor = [fold(jnp.broadcast_to(columns[:, d : d + 1], (heads, rest))) for d in range(n)]
        for step in steps:
            last_part_copy(i, step).wait_recv()
        first = sum(last_parts[d, i - main, :heads, :].astype(F32) * major[d] for d in range(n))
        second = sum(last_parts[d, i - main, heads:, :].astype(F32) * minor[d] for d in range(n))
        out_ref[i * heads : (i + 1) * heads, :LANES] = first.astype(BF16)
        out_ref[i * heads : (i + 1) * heads, LANES:] = unfold(second, rest).astype(BF16)

    row_ref[...] = jnp.zeros_like(row_ref)
    acc_ref[...] = jnp.zeros_like(acc_ref)
    w_ref[...] = jnp.zeros_like(w_ref)
    q_copy().wait()
    widen(0)
    k_copy(0).wait()
    s = scores(0)
    widen(1)
    weigh(0, s)
    k_copy(SLOTS).start()
    pl.semaphore_wait(barrier, n - 1)

    def attend(i):
        k_copy(i).wait()
        v_copy(i - 1).wait()
        s, acc = both(i)
        widen(i + 1)
        weigh(i, s)
        keep(i - 1, acc)

    def body(i, carry):
        attend(i)

        @pl.when(i + SLOTS < batch)
        def _():
            v_copy(i - 1 + SLOTS).start()

        @pl.when(i + SLOTS == batch)
        def _():
            for j in range(2):
                v_half(batch - 1, j).start()

        @pl.when(i + SLOTS < batch)
        def _():
            k_copy(i + SLOTS).start()

        @pl.when(lax.rem(i, pack) == 1)
        def _():
            send(chunk_of(i - 1))

        @pl.when((lax.rem(i, pack) == 0) & (i > 2 * pack))
        def _():
            combine(i // pack - 2)

        return carry

    lax.fori_loop(1, main, body, 0)
    for i in range(main, batch):
        k_copy(i).wait()
        v_copy(i - 1).wait()
        s, acc = both(i)
        if i + 1 < batch:
            widen(i + 1)
        keep(i - 1, acc)
        weigh(i, s)
        if i == main:
            send(chunks - 1)
    v_half(batch - 1, 0).wait()
    values(batch - 1, [v_half(batch - 1, 1)])

    def finish(c, carry):
        for step in steps:
            stat_copy(c, step).wait_send()
            part_copy(c, step).wait_send()
        return carry

    lax.fori_loop(0, chunks, finish, 0)
    combine(0)
    combine(chunks - 2)
    combine(chunks - 1)
    for i in range(main, batch):
        for step in steps:
            last_stat_copy(i, step).wait_send()
            last_part_copy(i, step).wait_send()
        combine_last(i)


def solution(mesh):
    axis = "sp"
    n = mesh.shape[axis]

    def step(q, k, v):
        batch, heads, head = q.shape
        run, kv_heads = k.shape[1], k.shape[2]
        flat = (batch, kv_heads * head, run)
        q = pltpu.with_memory_space_constraint(q, pltpu.HBM)
        k = k.transpose(0, 2, 3, 1).reshape(flat)
        v = v.transpose(0, 2, 3, 1).reshape(flat)
        pack = LANES // heads
        chunks, solo = batch // pack, pack - 1
        out = pl.pallas_call(
            functools.partial(kernel, axis, n, (batch, heads, kv_heads, head, run)),
            out_shape=jax.ShapeDtypeStruct((batch * heads, head), BF16),
            in_specs=[pl.BlockSpec(memory_space=pl.ANY)] * 3,
            out_specs=pl.BlockSpec(memory_space=pltpu.VMEM),
            scratch_shapes=[
                pltpu.VMEM((batch, heads, head), BF16),
                pltpu.VMEM((heads, kv_heads * head), BF16),
                pltpu.VMEM((SLOTS,) + flat[1:], BF16),
                pltpu.VMEM((SLOTS,) + flat[1:], BF16),
                pltpu.VMEM((LANES, run), BF16),
                pltpu.VMEM((head, LANES), F32),
                pltpu.VMEM((2, 8, LANES), F32),
                pltpu.VMEM((n, chunks, head, LANES), BF16),
                pltpu.VMEM((n, chunks, 8, LANES), F32),
                pltpu.VMEM((n, solo, heads * head // LANES, LANES), BF16),
                pltpu.VMEM((n, solo, 8, LANES), F32),
                pltpu.SemaphoreType.DMA,
                pltpu.SemaphoreType.DMA((SLOTS,)),
                pltpu.SemaphoreType.DMA((SLOTS,)),
                pltpu.SemaphoreType.DMA((2,)),
                pltpu.SemaphoreType.DMA((2, chunks, n - 1)),
                pltpu.SemaphoreType.DMA((2, chunks, n - 1)),
                pltpu.SemaphoreType.DMA((2, solo, n - 1)),
                pltpu.SemaphoreType.DMA((2, solo, n - 1)),
            ],
            compiler_params=pltpu.CompilerParams(collective_id=0, has_side_effects=True, vmem_limit_bytes=VMEM_LIMIT),
        )(q, k, v)
        return out.reshape(q.shape)

    return jax.shard_map(
        step,
        mesh=mesh,
        in_specs=(P("dp", None, None), P("dp", "sp", None, None), P("dp", "sp", None, None)),
        out_specs=P("dp", None, None),
        check_vma=False,
    )
```

time: 62.2 us -> 60.2 us (0.968)
  local copies, waits for them, and re-layouts: 1.87 us -> 0.8 us
  Pallas kernels: 60.1 us -> 59.3 us
    unnamed x1, local copies, waits for them, and re-layouts: 1.87 us -> 0.8 us
    pallas_call x1, Pallas kernels: 60.1 us -> 59.3 us  [step(): pl.pallas_call(functools.partial(kernel, axis, n, (batch, heads, kv_heads...]
where the time goes in v2:
time: 60.2 us; the launch traced here: 60.1 us
  Pallas kernels  59.3 us (99%)
  local copies, waits for them, and re-layouts  0.8 us (1%)
    pallas_call x1, Pallas kernels, step(): pl.pallas_call(functools.partial(kernel, axis, n, (batch, heads, kv_heads...  59.3 us

profile of v2, /device:TPU:112, one launch (start us, length us, event | category | flops | bytes accessed | tf_op | source)
XLA Modules:
  0.0 60.1 jit_solution(1367150722015752817)
XLA Ops:
  0.0 59.3 %shard_map.37 = bf16[1024,160]{1,0:T(8,128)(2,1)S(1)} custom-call(bf16[32,32,160]{2,1,0:T(8,128)(2,1)} %q_hbm.1, bf16[32,1280,1024]{2,1,0:T(8,128)(2,1)} %bitcast.1.k_hbm, bf16[32,1280,1024]{2,1,0:T(8,128)(2,1)} %bitcast.3.v_hbm), custom_call_target="tpu_custom_call" | custom-call | tf_op jit(solution)/shard_map/pallas_call | solution.py:306
  59.3 0.8 %copy.5 = bf16[32,32,160]{2,1,0:T(8,128)(2,1)} copy(bf16[32,32,160]{2,1,0:T(8,128)(2,1)S(1)} %bitcast.7) | data formatting | bytes 655360
